TPU v7x, 32 devices: a whole 2x2x4 slice. The times are simulated.
32 devices in a mesh: gx: 4 (over y, x), gy: 2 (over core), gz: 4 (over z).
Axes of the slice: x: 2, y: 2, z: 4, core: 2. Of those that a mesh axis runs over, the one named last changes fastest.
Arguments:
- gradient: bfloat16 [32, 32, 16, 512], P(None, 'gx', 'gy', 'gz'), may hold values from -6 to 6
- noise_draw: bfloat16 [32, 32, 16, 512], P(None, 'gx', 'gy', 'gz'), may hold values from -6 to 6
- current: float32 [32, 32, 16, 512], P(None, 'gx', 'gy', 'gz'), may hold values from -6 to 6
- eigvectors: bfloat16 [32, 16, 512, 512], P('gx', 'gy', 'gz'), may hold values from -0.125 to 0.125
- eigvalues: float32 [512], replicated, may hold values from 0.05 to 50
- reaction: float32 [32, 16, 512], P('gx', 'gy', 'gz'), may hold values from 0.25 to 4
Outputs:
- proposal: float32 [32, 32, 16, 512], P(None, 'gx', 'gy', 'gz')
All inputs are finite; a program needn't handle non-finite values.
Results may differ from a plain program's by a relative error of at most 0.00031.
Values sent between devices are 32-bit elements; how exact they have to be, the bound alone decides.
A program may use at most 64 MiB of HBM per device.

v0:
```python
import jax
import jax.numpy as jnp
from jax import lax
from jax.sharding import PartitionSpec as P

SWEEPS = 4


def with_halo(block, sides, width):
    for axis, dim in sides:
        count = lax.axis_size(axis)
        forward = [(i, i + 1) for i in range(count - 1)]
        backward = [(target, source) for source, target in forward]
        low = lax.ppermute(
            lax.slice_in_dim(block, block.shape[dim] - width, None, axis=dim), axis, forward
        )
        high = lax.ppermute(lax.slice_in_dim(block, 0, width, axis=dim), axis, backward)
        block = jnp.concatenate([low, block, high], axis=dim)
    return block


def prior_root(source, reaction):
    sweeps = SWEEPS
    diagonal = reaction + 6.0
    field = source / diagonal
    for sweep_index in range(sweeps - 1):
        padded = with_halo(field, (("gx", 1), ("gy", 2), ("gz", 3)), 1)
        total = padded[:, 2:, 1:-1, 1:-1] + padded[:, :-2, 1:-1, 1:-1]
        total = total + padded[:, 1:-1, 2:, 1:-1] + padded[:, 1:-1, :-2, 1:-1]
        total = total + padded[:, 1:-1, 1:-1, 2:] + padded[:, 1:-1, 1:-1, :-2]
        field = (source + total) / diagonal
    return field


def body(gradient, noise_draw, current, eigvectors, eigvalues, reaction):
    chains = gradient.shape[0]
    rank = eigvectors.shape[3]
    cells = reaction.shape[0] * reaction.shape[1] * reaction.shape[2]
    basis = eigvectors.reshape(cells, rank)
    stacked = jnp.concatenate(
        [gradient.reshape(chains, cells), noise_draw.reshape(chains, cells)], 0
    )
    partial_sums = jnp.dot(stacked, basis, preferred_element_type=jnp.float32)
    local_part = -0.5 * gradient.astype(jnp.float32) + 1.0 * noise_draw.astype(jnp.float32)
    sums = lax.psum(partial_sums, ("gx", "gy", "gz"))
    damp = eigvalues / (eigvalues + 1.0)
    root_damp = 1.0 - 1.0 / jnp.sqrt(1.0 + eigvalues)
    coef = (0.5 * damp * sums[:chains] - 1.0 * root_damp * sums[chains:]).astype(jnp.bfloat16)
    corr = lax.dot_general(
        coef, basis, (((1,), (1,)), ((), ())), preferred_element_type=jnp.float32
    )
    field = prior_root(local_part + corr.reshape(current.shape), reaction)
    return current + field


def solution(mesh):
    return jax.shard_map(
        body,
        mesh=mesh,
        in_specs=(
            P(None, "gx", "gy", "gz"),
            P(None, "gx", "gy", "gz"),
            P(None, "gx", "gy", "gz"),
            P("gx", "gy", "gz", None),
            P(),
            P("gx", "gy", "gz"),
        ),
        out_specs=P(None, "gx", "gy", "gz"),
        check_vma=False,
    )
```

profile of v0, /device:TPU:0, one launch (start us, length us, event | category | flops | bytes accessed | tf_op | source)
XLA Modules:
  0.0 262.8 jit_solution(8625238853567087662)
XLA Ops:
  6.5 1.9 copy_bitcast_fusion
  8.4 5.7 %fusion.22 = f32[64,512]{1,0:T(8,128)} fusion(bf16[8192,512]{1,0:T(8,128)(2,1)} %bitcast.18, bf16[32,8192]{1,0:T(8,128)(2,1)S(1)} %get-tuple-element.27, bf16[32,8192]{1,0:T(8,128)(2,1)S(1)} %get-tuple-element.28), kind=kOutput, calls=%fused_computation.80 | convolution fusion | flops 538968064 | bytes 9568256 | tf_op jit(solution)/shard_map/dot_general | solution.py:43
  14.2 127.2 %all-reduce.2.cloned.1.call-done = f32[64,512]{1,0:T(8,128)} async-done(((f32[64,512]{1,0:T(8,128)}), f32[64,512]{1,0:T(8,128)}) %all-reduce.2.cloned.1.call-update) | async-done | bytes 131088 | tf_op jit(solution)/shard_map/psum | solution.py:45
  141.5 6.0 %broadcast_divide_fusion = (f32[32,8,8,128]{3,0,2,1:T(8,128)S(1)}, f32[32,8,8,128]{3,0,2,1:T(8,128)S(1)}) fusion(f32[8,8,128]{2,1,0:T(8,128)S(1)} %broadcast_add_fusion, bf16[8,8,128,512]{3,2,1,0:T(8,128)(2,1)} %param.9, f32[64,512]{1,0:T(8,128)} %all-reduce.2.cloned.1.call-done, f32[512]{0:T(512)S(1)} %get-tuple-element.24, f32[512]{0:T(512)S(1)} %get-tuple-element.23, ...), kind=kOutput, calls=%fused_computation.86 | convolution fusion | flops 270073856 | bytes 11702272 | tf_op jit(solution)/shard_map/dot_general | solution.py:49
  147.5 3.4 %collective-permute-start.1 = (f32[32,1,8,128]{3,0,2,1:T(8,128)S(1)}, f32[32,1,8,128]{3,0,2,1:T(8,128)S(1)}, u32[]{:S(2)}, u32[]{:S(2)}) collective-permute-start(f32[32,1,8,128]{3,0,2,1:T(8,128)S(1)} %get-tuple-element.21), channel_id=1, source_target_pairs={{0,8},{8,16},{16,24},{1,9},{9,17},{17,25},{2,10},{10,18},{18,26},{... | collective-permute-start | bytes 393224 | tf_op jit(solution)/shard_map/ppermute | solution.py:14
  153.4 4.7 %collective-permute-done = f32[32,1,8,128]{3,0,2,1:T(8,128)S(1)} collective-permute-done((f32[32,1,8,128]{3,0,2,1:T(8,128)S(1)}, f32[32,1,8,128]{3,0,2,1:T(8,128)S(1)}, u32[]{:S(2)}, u32[]{:S(2)}) %collective-permute-start) | collective-permute-done | bytes 131104 | tf_op jit(solution)/shard_map/ppermute | solution.py:17
  160.8 2.0 collective-permute-done.2
  163.4 2.3 fusion.37
  165.7 2.1 copy.13
  169.0 2.1 copy.15
  171.1 4.6 %collective-permute-start.5 = (f32[32,10,10,1]{0,3,2,1:T(1,128)S(1)}, f32[32,10,10,1]{0,3,2,1:T(1,128)S(1)}, u32[]{:S(2)}, u32[]{:S(2)}) collective-permute-start(f32[32,10,10,1]{0,3,2,1:T(1,128)S(1)} %copy.15), channel_id=1, source_target_pairs={{0,1},{1,2},{2,3},{4,5},{5,6},{6,7},{8,9},{9,10},{10,11},{12,13},{... | collective-permute-start | bytes 38408 | tf_op jit(solution)/shard_map/ppermute | solution.py:14
  177.5 1.9 copy.16
  179.4 2.9 %fusion.17 = f32[32,8,8,128]{3,0,2,1:T(8,128)S(1)} fusion(f32[32,8,8,128]{3,0,2,1:T(8,128)S(1)} %get-tuple-element.26, f32[32,10,10,1]{3,0,2,1:T(8,128)} %copy.16, f32[32,10,1,128]{3,0,2,1:T(8,128)} %copy-done.5, f32[32,10,1,128]{3,0,2,1:T(8,128)} %copy-done.3, f32[32,1,8,128]{3,0,2,1:T(8,128)S(1)} %collective-permute-done, ...), kind=kLoop, calls=%fused_computation.58 | loop fusion | flops 6553600 | bytes 3793920 | tf_op jit(solution)/shard_map/div | solution.py:31
  182.3 3.9 %collective-permute-start.7 = (f32[32,1,8,128]{3,0,2,1:T(8,128)S(1)}, f32[32,1,8,128]{3,0,2,1:T(8,128)S(1)}, u32[]{:S(2)}, u32[]{:S(2)}) collective-permute-start(f32[32,1,8,128]{3,0,2,1:T(8,128)S(1)} %get-tuple-element.19), channel_id=1, source_target_pairs={{0,8},{8,16},{16,24},{1,9},{9,17},{17,25},{2,10},{10,18},{18,26},{... | collective-permute-start | bytes 393224 | tf_op jit(solution)/shard_map/ppermute | solution.py:14
  188.8 4.4 %collective-permute-done.6 = f32[32,1,8,128]{3,0,2,1:T(8,128)S(1)} collective-permute-done((f32[32,1,8,128]{3,0,2,1:T(8,128)S(1)}, f32[32,1,8,128]{3,0,2,1:T(8,128)S(1)}, u32[]{:S(2)}, u32[]{:S(2)}) %collective-permute-start.6) | collective-permute-done | bytes 131104 | tf_op jit(solution)/shard_map/ppermute | solution.py:17
  195.8 2.0 collective-permute-done.8
  198.4 2.3 fusion.36
  200.7 2.1 copy.17
  204.0 2.1 copy.19
  206.1 4.8 %collective-permute-start.11 = (f32[32,10,10,1]{0,3,2,1:T(1,128)S(1)}, f32[32,10,10,1]{0,3,2,1:T(1,128)S(1)}, u32[]{:S(2)}, u32[]{:S(2)}) collective-permute-start(f32[32,10,10,1]{0,3,2,1:T(1,128)S(1)} %copy.19), channel_id=1, source_target_pairs={{0,1},{1,2},{2,3},{4,5},{5,6},{6,7},{8,9},{9,10},{10,11},{12,13},{... | collective-permute-start | bytes 38408 | tf_op jit(solution)/shard_map/ppermute | solution.py:14
  212.8 1.9 copy.20
  214.6 2.9 %fusion.10 = f32[32,8,8,128]{3,0,2,1:T(8,128)S(1)} fusion(f32[32,8,8,128]{3,0,2,1:T(8,128)S(1)} %get-tuple-element.26, f32[32,10,10,1]{3,0,2,1:T(8,128)} %copy.20, f32[32,10,1,128]{3,0,2,1:T(8,128)} %copy-done.6, f32[32,10,1,128]{3,0,2,1:T(8,128)} %copy-done.4, f32[32,1,8,128]{3,0,2,1:T(8,128)S(1)} %collective-permute-done.6, ...), kind=kLoop, calls=%fused_computation.33 | loop fusion | flops 6553600 | bytes 3793920 | tf_op jit(solution)/shard_map/div | solution.py:31
  217.5 3.4 %collective-permute-start.13 = (f32[32,1,8,128]{3,0,2,1:T(8,128)S(1)}, f32[32,1,8,128]{3,0,2,1:T(8,128)S(1)}, u32[]{:S(2)}, u32[]{:S(2)}) collective-permute-start(f32[32,1,8,128]{3,0,2,1:T(8,128)S(1)} %get-tuple-element.17), channel_id=1, source_target_pairs={{0,8},{8,16},{16,24},{1,9},{9,17},{17,25},{2,10},{10,18},{18,26},{... | collective-permute-start | bytes 393224 | tf_op jit(solution)/shard_map/ppermute | solution.py:14
  223.7 4.1 %collective-permute-done.12 = f32[32,1,8,128]{3,0,2,1:T(8,128)S(1)} collective-permute-done((f32[32,1,8,128]{3,0,2,1:T(8,128)S(1)}, f32[32,1,8,128]{3,0,2,1:T(8,128)S(1)}, u32[]{:S(2)}, u32[]{:S(2)}) %collective-permute-start.12) | collective-permute-done | bytes 131104 | tf_op jit(solution)/shard_map/ppermute | solution.py:17
  230.5 2.0 collective-permute-done.14
  233.1 2.2 fusion.35
  235.3 2.1 copy.21
  238.7 2.7 %copy.23 = f32[32,10,10,1]{0,3,2,1:T(1,128)} copy(f32[32,10,10,1]{3,0,2,1:T(8,128)} %get-tuple-element.6) | data formatting | bytes 25600 | tf_op jit(solution)/shard_map/slice | solution.py:15
  241.4 5.5 %collective-permute-start.17 = (f32[32,10,10,1]{0,3,2,1:T(1,128)}, f32[32,10,10,1]{0,3,2,1:T(1,128)}, u32[]{:S(2)}, u32[]{:S(2)}) collective-permute-start(f32[32,10,10,1]{0,3,2,1:T(1,128)} %copy.23), channel_id=1, source_target_pairs={{0,1},{1,2},{2,3},{4,5},{5,6},{6,7},{8,9},{9,10},{10,11},{12,13},{... | collective-permute-start | bytes 38408 | tf_op jit(solution)/shard_map/ppermute | solution.py:14
  246.9 1.9 copy.22
  248.8 2.6 %copy.24 = f32[32,10,10,1]{3,0,2,1:T(8,128)} copy(f32[32,10,10,1]{0,3,2,1:T(1,128)} %collective-permute-done.17) | data formatting | bytes 25600 | tf_op jit(solution)/shard_map/ppermute | solution.py:14
  251.4 3.0 %fusion.3 = f32[32,8,8,128]{3,0,2,1:T(8,128)S(1)} fusion(f32[32,8,8,128]{3,0,2,1:T(8,128)S(1)} %get-tuple-element.26, f32[32,10,10,1]{3,0,2,1:T(8,128)} %copy.24, f32[32,10,1,128]{3,0,2,1:T(8,128)} %copy-done.8, f32[32,10,1,128]{3,0,2,1:T(8,128)} %copy-done.7, f32[32,1,8,128]{3,0,2,1:T(8,128)S(1)} %collective-permute-done.12, ...), kind=kLoop, calls=%fused_computation.8 | loop fusion | flops 6815744 | bytes 4842496 | tf_op jit(solution)/shard_map/add | solution.py:53
  (62 shorter events, 26.8 us)
Async XLA Ops:
  6.5 134.9 %all-reduce.2.cloned.1.call-start = ((), (), s32[]{:S(2)}) async-start(), calls=%async_computation | async-start | bytes 262144 | tf_op jit(solution)/shard_map/psum | solution.py:45
  8.4 5.8 %copy-start.9 = (f32[8,8,128]{2,1,0:T(8,128)S(1)}, f32[8,8,128]{2,1,0:T(8,128)}, u32[]{:S(2)}) copy-start(f32[8,8,128]{2,1,0:T(8,128)} %param.11) | copy-start | bytes 98308
  8.4 5.8 %copy-start.10 = (f32[512]{0:T(512)S(1)}, f32[512]{0:T(512)}, u32[]{:S(2)}) copy-start(f32[512]{0:T(512)} %param.10) | copy-start | bytes 6148
  8.4 133.0 %copy-start = (bf16[32,8,8,128]{3,2,1,0:T(8,128)(2,1)S(1)}, bf16[32,8,8,128]{3,2,1,0:T(8,128)(2,1)}, u32[]{:S(2)}) copy-start(bf16[32,8,8,128]{3,2,1,0:T(8,128)(2,1)} %param.7) | copy-start | bytes 1572868
  8.4 133.0 %copy-start.1 = (bf16[32,8,8,128]{3,2,1,0:T(8,128)(2,1)S(1)}, bf16[32,8,8,128]{3,2,1,0:T(8,128)(2,1)}, u32[]{:S(2)}) copy-start(bf16[32,8,8,128]{3,2,1,0:T(8,128)(2,1)} %param.6) | copy-start | bytes 1572868
  147.5 5.9 %collective-permute-start.1 = (f32[32,1,8,128]{3,0,2,1:T(8,128)S(1)}, f32[32,1,8,128]{3,0,2,1:T(8,128)S(1)}, u32[]{:S(2)}, u32[]{:S(2)}) collective-permute-start(f32[32,1,8,128]{3,0,2,1:T(8,128)S(1)} %get-tuple-element.21), channel_id=1, source_target_pairs={{0,8},{8,16},{16,24},{1,9},{9,17},{17,25},{2,10},{10,18},{18,26},{... | collective-permute-start | bytes 393224 | tf_op jit(solution)/shard_map/ppermute | solution.py:14
  150.9 7.2 %collective-permute-start = (f32[32,1,8,128]{3,0,2,1:T(8,128)S(1)}, f32[32,1,8,128]{3,0,2,1:T(8,128)S(1)}, u32[]{:S(2)}, u32[]{:S(2)}) collective-permute-start(f32[32,1,8,128]{3,0,2,1:T(8,128)S(1)} %get-tuple-element.22), channel_id=1, source_target_pairs={{8,0},{16,8},{24,16},{9,1},{17,9},{25,17},{10,2},{18,10},{26,18},{... | collective-permute-start | bytes 393224 | tf_op jit(solution)/shard_map/ppermute | solution.py:17
  158.1 2.6 collective-permute-start.3
  159.5 3.3 %collective-permute-start.2 = (f32[32,10,1,128]{3,0,2,1:T(8,128)S(1)}, f32[32,10,1,128]{3,0,2,1:T(8,128)S(1)}, u32[]{:S(2)}, u32[]{:S(2)}) collective-permute-start(f32[32,10,1,128]{3,0,2,1:T(8,128)S(1)} %get-tuple-element.16), channel_id=1, source_target_pairs={{4,0},{5,1},{6,2},{7,3},{12,8},{13,9},{14,10},{15,11},{20,16},{21,... | collective-permute-start | bytes 491528 | tf_op jit(solution)/shard_map/ppermute | solution.py:17
  160.8 2.2 copy-start.3
  162.7 0.7 copy-start.5
  167.7 7.9 %collective-permute-start.4 = (f32[32,10,10,1]{0,3,2,1:T(1,128)S(1)}, f32[32,10,10,1]{0,3,2,1:T(1,128)S(1)}, u32[]{:S(2)}, u32[]{:S(2)}) collective-permute-start(f32[32,10,10,1]{0,3,2,1:T(1,128)S(1)} %copy.13), channel_id=1, source_target_pairs={{1,0},{2,1},{3,2},{5,4},{6,5},{7,6},{9,8},{10,9},{11,10},{13,12},{... | collective-permute-start | bytes 38408 | tf_op jit(solution)/shard_map/ppermute | solution.py:17
  171.1 6.4 %collective-permute-start.5 = (f32[32,10,10,1]{0,3,2,1:T(1,128)S(1)}, f32[32,10,10,1]{0,3,2,1:T(1,128)S(1)}, u32[]{:S(2)}, u32[]{:S(2)}) collective-permute-start(f32[32,10,10,1]{0,3,2,1:T(1,128)S(1)} %copy.15), channel_id=1, source_target_pairs={{0,1},{1,2},{2,3},{4,5},{5,6},{6,7},{8,9},{9,10},{10,11},{12,13},{... | collective-permute-start | bytes 38408 | tf_op jit(solution)/shard_map/ppermute | solution.py:14
  182.3 6.4 %collective-permute-start.7 = (f32[32,1,8,128]{3,0,2,1:T(8,128)S(1)}, f32[32,1,8,128]{3,0,2,1:T(8,128)S(1)}, u32[]{:S(2)}, u32[]{:S(2)}) collective-permute-start(f32[32,1,8,128]{3,0,2,1:T(8,128)S(1)} %get-tuple-element.19), channel_id=1, source_target_pairs={{0,8},{8,16},{16,24},{1,9},{9,17},{17,25},{2,10},{10,18},{18,26},{... | collective-permute-start | bytes 393224 | tf_op jit(solution)/shard_map/ppermute | solution.py:14
  186.3 6.9 %collective-permute-start.6 = (f32[32,1,8,128]{3,0,2,1:T(8,128)S(1)}, f32[32,1,8,128]{3,0,2,1:T(8,128)S(1)}, u32[]{:S(2)}, u32[]{:S(2)}) collective-permute-start(f32[32,1,8,128]{3,0,2,1:T(8,128)S(1)} %get-tuple-element.20), channel_id=1, source_target_pairs={{8,0},{16,8},{24,16},{9,1},{17,9},{25,17},{10,2},{18,10},{26,18},{... | collective-permute-start | bytes 393224 | tf_op jit(solution)/shard_map/ppermute | solution.py:17
  193.2 2.6 collective-permute-start.9
  194.5 3.3 %collective-permute-start.8 = (f32[32,10,1,128]{3,0,2,1:T(8,128)S(1)}, f32[32,10,1,128]{3,0,2,1:T(8,128)S(1)}, u32[]{:S(2)}, u32[]{:S(2)}) collective-permute-start(f32[32,10,1,128]{3,0,2,1:T(8,128)S(1)} %get-tuple-element.14), channel_id=1, source_target_pairs={{4,0},{5,1},{6,2},{7,3},{12,8},{13,9},{14,10},{15,11},{20,16},{21,... | collective-permute-start | bytes 491528 | tf_op jit(solution)/shard_map/ppermute | solution.py:17
  195.8 2.2 copy-start.4
  197.8 0.7 copy-start.6
  202.7 8.2 %collective-permute-start.10 = (f32[32,10,10,1]{0,3,2,1:T(1,128)S(1)}, f32[32,10,10,1]{0,3,2,1:T(1,128)S(1)}, u32[]{:S(2)}, u32[]{:S(2)}) collective-permute-start(f32[32,10,10,1]{0,3,2,1:T(1,128)S(1)} %copy.17), channel_id=1, source_target_pairs={{1,0},{2,1},{3,2},{5,4},{6,5},{7,6},{9,8},{10,9},{11,10},{13,12},{... | collective-permute-start | bytes 38408 | tf_op jit(solution)/shard_map/ppermute | solution.py:17
  206.1 6.6 %collective-permute-start.11 = (f32[32,10,10,1]{0,3,2,1:T(1,128)S(1)}, f32[32,10,10,1]{0,3,2,1:T(1,128)S(1)}, u32[]{:S(2)}, u32[]{:S(2)}) collective-permute-start(f32[32,10,10,1]{0,3,2,1:T(1,128)S(1)} %copy.19), channel_id=1, source_target_pairs={{0,1},{1,2},{2,3},{4,5},{5,6},{6,7},{8,9},{9,10},{10,11},{12,13},{... | collective-permute-start | bytes 38408 | tf_op jit(solution)/shard_map/ppermute | solution.py:14
  217.5 6.1 %collective-permute-start.13 = (f32[32,1,8,128]{3,0,2,1:T(8,128)S(1)}, f32[32,1,8,128]{3,0,2,1:T(8,128)S(1)}, u32[]{:S(2)}, u32[]{:S(2)}) collective-permute-start(f32[32,1,8,128]{3,0,2,1:T(8,128)S(1)} %get-tuple-element.17), channel_id=1, source_target_pairs={{0,8},{8,16},{16,24},{1,9},{9,17},{17,25},{2,10},{10,18},{18,26},{... | collective-permute-start | bytes 393224 | tf_op jit(solution)/shard_map/ppermute | solution.py:14
  220.9 6.9 %collective-permute-start.12 = (f32[32,1,8,128]{3,0,2,1:T(8,128)S(1)}, f32[32,1,8,128]{3,0,2,1:T(8,128)S(1)}, u32[]{:S(2)}, u32[]{:S(2)}) collective-permute-start(f32[32,1,8,128]{3,0,2,1:T(8,128)S(1)} %get-tuple-element.18), channel_id=1, source_target_pairs={{8,0},{16,8},{24,16},{9,1},{17,9},{25,17},{10,2},{18,10},{26,18},{... | collective-permute-start | bytes 393224 | tf_op jit(solution)/shard_map/ppermute | solution.py:17
  227.8 2.6 collective-permute-start.15
  229.1 3.3 %collective-permute-start.14 = (f32[32,10,1,128]{3,0,2,1:T(8,128)S(1)}, f32[32,10,1,128]{3,0,2,1:T(8,128)S(1)}, u32[]{:S(2)}, u32[]{:S(2)}) collective-permute-start(f32[32,10,1,128]{3,0,2,1:T(8,128)S(1)} %get-tuple-element.12), channel_id=1, source_target_pairs={{4,0},{5,1},{6,2},{7,3},{12,8},{13,9},{14,10},{15,11},{20,16},{21,... | collective-permute-start | bytes 491528 | tf_op jit(solution)/shard_map/ppermute | solution.py:17
  230.4 2.2 copy-start.7
  232.4 0.7 copy-start.8
  237.4 9.5 %collective-permute-start.16 = (f32[32,10,10,1]{0,3,2,1:T(1,128)S(1)}, f32[32,10,10,1]{0,3,2,1:T(1,128)S(1)}, u32[]{:S(2)}, u32[]{:S(2)}) collective-permute-start(f32[32,10,10,1]{0,3,2,1:T(1,128)S(1)} %copy.21), channel_id=1, source_target_pairs={{1,0},{2,1},{3,2},{5,4},{6,5},{7,6},{9,8},{10,9},{11,10},{13,12},{... | collective-permute-start | bytes 38408 | tf_op jit(solution)/shard_map/ppermute | solution.py:17
  241.4 10.0 %copy-start.2 = (f32[32,8,8,128]{3,2,1,0:T(8,128)S(1)}, f32[32,8,8,128]{3,2,1,0:T(8,128)}, u32[]{:S(2)}) copy-start(f32[32,8,8,128]{3,2,1,0:T(8,128)} %param.8) | copy-start | bytes 3145732
  241.4 7.4 %collective-permute-start.17 = (f32[32,10,10,1]{0,3,2,1:T(1,128)}, f32[32,10,10,1]{0,3,2,1:T(1,128)}, u32[]{:S(2)}, u32[]{:S(2)}) collective-permute-start(f32[32,10,10,1]{0,3,2,1:T(1,128)} %copy.23), channel_id=1, source_target_pairs={{0,1},{1,2},{2,3},{4,5},{5,6},{6,7},{8,9},{9,10},{10,11},{12,13},{... | collective-permute-start | bytes 38408 | tf_op jit(solution)/shard_map/ppermute | solution.py:14
Sparse Core Ops, SparseCore 0:
  14.3 127.1 all-reduce.1
where the time goes:
time: 264 us; the launch traced here: 263 us
  waiting for transfers between devices  150 us (57%)
  starting transfers between devices  41.1 us (16%)
  local copies, waits for them, and re-layouts  36.7 us (14%)
  between operations  13.8 us (5%)
  matrix products  11.7 us (4%)
  other arithmetic  9.37 us (4%)
    psum x1, waiting for transfers between devices, body(): sums = lax.psum(partial_sums, ('gx', 'gy', 'gz'))  127 us
    ppermute x9, starting transfers between devices, with_halo(): lax.ppermute(lax.slice_in_dim(block, block.shape[dim] - width, None, axis...  29.4 us
    ppermute x9, waiting for transfers between devices, with_halo(): lax.ppermute(lax.slice_in_dim(block, 0, width, axis=dim), axis, backward)  19.1 us
    slice x6, local copies, waits for them, and re-layouts, with_halo(): lax.slice_in_dim(block, 0, width, axis=dim)  13 us
    ppermute x9, starting transfers between devices, with_halo(): lax.ppermute(lax.slice_in_dim(block, 0, width, axis=dim), axis, backward)  11.6 us
    slice x6, local copies, waits for them, and re-layouts, with_halo(): lax.slice_in_dim(block, block.shape[dim] - width, None, axis=dim)  6.9 us
    ppermute x3, local copies, waits for them, and re-layouts, with_halo(): lax.ppermute(lax.slice_in_dim(block, block.shape[dim] - width, None, axis...  6.34 us
    dot_general x1, matrix products, body(): lax.dot_general(coef, basis, (((1,), (1,)), ((), ())), preferred_element_...  6.04 us
  transfers between devices with their start and end apart: 19, of which 10 were waited for; matrix products, arithmetic and copies ran while one was open for 5% of the time, Pallas kernels for 0%

commit v1 on v0

--- a/solution.py
+++ b/solution.py
@@ -42,7 +42,8 @@
     )
     partial_sums = jnp.dot(stacked, basis, preferred_element_type=jnp.float32)
     local_part = -0.5 * gradient.astype(jnp.float32) + 1.0 * noise_draw.astype(jnp.float32)
-    sums = lax.psum(partial_sums, ("gx", "gy", "gz"))
+    point_paths_here = lambda inputs, peer_axis: jnp.sum(lax.all_gather(inputs, peer_axis), axis=0)
+    sums = point_paths_here(partial_sums, ("gx", "gy", "gz"))
     damp = eigvalues / (eigvalues + 1.0)
     root_damp = 1.0 - 1.0 / jnp.sqrt(1.0 + eigvalues)
     coef = (0.5 * damp * sums[:chains] - 1.0 * root_damp * sums[chains:]).astype(jnp.bfloat16)

time: 264 us -> 204 us (0.77)
  waiting for transfers between devices: 150 us -> 88.3 us
    psum x1 -> x0, waiting for transfers between devices: 127 us -> none  [body(): sums = lax.psum(partial_sums, ('gx', 'gy', 'gz'))]
    all_gather x0 -> x1, waiting for transfers between devices: none -> 64.5 us  [body(): lax.all_gather(inputs, peer_axis)]
  transfers between devices with their start and end apart: 19 -> 19, of which waited for: 10 -> 10; matrix products, arithmetic and copies ran while one was open for 5% -> 6% of each run, Pallas kernels for 0% -> 0%
where the time goes in v1:
time: 204 us; the launch traced here: 203 us
  waiting for transfers between devices  88.3 us (43%)
  starting transfers between devices  40.2 us (20%)
  local copies, waits for them, and re-layouts  36.8 us (18%)
  between operations  13.8 us (7%)
  other arithmetic  12 us (6%)
  matrix products  11.6 us (6%)
    all_gather x1, waiting for transfers between devices, body(): lax.all_gather(inputs, peer_axis)  64.5 us
    ppermute x9, starting transfers between devices, with_halo(): lax.ppermute(lax.slice_in_dim(block, block.shape[dim] - width, None, axis...  28.4 us
    ppermute x9, waiting for transfers between devices, with_halo(): lax.ppermute(lax.slice_in_dim(block, 0, width, axis=dim), axis, backward)  19.3 us
    slice x6, local copies, waits for them, and re-layouts, with_halo(): lax.slice_in_dim(block, 0, width, axis=dim)  13 us
    ppermute x9, starting transfers between devices, with_halo(): lax.ppermute(lax.slice_in_dim(block, 0, width, axis=dim), axis, backward)  11.8 us
    slice x6, local copies, waits for them, and re-layouts, with_halo(): lax.slice_in_dim(block, block.shape[dim] - width, None, axis=dim)  6.9 us
    ppermute x3, local copies, waits for them, and re-layouts, with_halo(): lax.ppermute(lax.slice_in_dim(block, block.shape[dim] - width, None, axis...  6.34 us
    dot_general x1, matrix products, body(): lax.dot_general(coef, basis, (((1,), (1,)), ((), ())), preferred_element_...  5.97 us
  transfers between devices with their start and end apart: 19, of which 10 were waited for; matrix products, arithmetic and copies ran while one was open for 6% of the time, Pallas kernels for 0%

profile of v1, /device:TPU:0, one launch (start us, length us, event | category | flops | bytes accessed | tf_op | source)
XLA Modules:
  0.0 202.7 jit_solution(388564324414151335)
XLA Ops:
  6.5 1.9 copy_bitcast_fusion
  8.4 5.6 %fusion.22 = f32[64,512]{1,0:T(8,128)} fusion(bf16[8192,512]{1,0:T(8,128)(2,1)} %bitcast.19, bf16[32,8192]{1,0:T(8,128)(2,1)S(1)} %get-tuple-element.27, bf16[32,8192]{1,0:T(8,128)(2,1)S(1)} %get-tuple-element.28), kind=kOutput, calls=%fused_computation.80 | convolution fusion | flops 538968064 | bytes 9568256 | tf_op jit(solution)/shard_map/dot_general | solution.py:43
  14.1 64.5 %all-gather.3.cloned.1.call-done = f32[2048,512]{1,0:T(8,128)} async-done(((f32[64,512]{1,0:T(8,128)}), f32[2048,512]{1,0:T(8,128)}) %all-gather.3.cloned.1.call-update) | async-done | bytes 4194320 | tf_op jit(solution)/shard_map/all_gather | solution.py:45
  78.6 2.6 %reduce_sum.9 = f32[64,512]{1,0:T(8,128)S(1)} reduce(f32[32,64,512]{2,1,0:T(8,128)} %bitcast.20, f32[]{:T(128)} %constant.3.clone.1), dimensions={0}, to_apply=%region_0.0 | reduce | flops 1015808 | bytes 4325380 | tf_op jit(solution)/shard_map/reduce_sum | solution.py:45
  81.2 6.0 %broadcast_divide_fusion = (f32[32,8,8,128]{3,0,2,1:T(8,128)S(1)}, f32[32,8,8,128]{3,0,2,1:T(8,128)S(1)}) fusion(f32[8,8,128]{2,1,0:T(8,128)S(1)} %broadcast_add_fusion, bf16[8,8,128,512]{3,2,1,0:T(8,128)(2,1)} %param.9, f32[64,512]{1,0:T(8,128)S(1)} %reduce_sum.9, f32[512]{0:T(512)S(1)} %get-tuple-element.24, f32[512]{0:T(512)S(1)} %get-tuple-element.23, ...), kind=kOutput, calls=%fused_computation.86 | convolution fusion | flops 270073856 | bytes 11702272 | tf_op jit(solution)/shard_map/dot_general | solution.py:50
  87.2 3.2 %collective-permute-start.1 = (f32[32,1,8,128]{3,0,2,1:T(8,128)S(1)}, f32[32,1,8,128]{3,0,2,1:T(8,128)S(1)}, u32[]{:S(2)}, u32[]{:S(2)}) collective-permute-start(f32[32,1,8,128]{3,0,2,1:T(8,128)S(1)} %get-tuple-element.21), channel_id=1, source_target_pairs={{0,8},{8,16},{16,24},{1,9},{9,17},{17,25},{2,10},{10,18},{18,26},{... | collective-permute-start | bytes 393224 | tf_op jit(solution)/shard_map/ppermute | solution.py:14
  93.5 4.9 %collective-permute-done = f32[32,1,8,128]{3,0,2,1:T(8,128)S(1)} collective-permute-done((f32[32,1,8,128]{3,0,2,1:T(8,128)S(1)}, f32[32,1,8,128]{3,0,2,1:T(8,128)S(1)}, u32[]{:S(2)}, u32[]{:S(2)}) %collective-permute-start) | collective-permute-done | bytes 131104 | tf_op jit(solution)/shard_map/ppermute | solution.py:17
  101.1 2.0 collective-permute-done.2
  103.8 2.3 %fusion.37 = (f32[32,10,10,1]{3,0,2,1:T(8,128)}, f32[32,10,10,1]{3,0,2,1:T(8,128)}) fusion(f32[32,10,10,128]{3,0,2,1:T(8,128)S(1)} %pad_maximum_fusion), kind=kLoop, calls=%fused_computation.111 | loop fusion | bytes 51200 | tf_op jit(solution)/shard_map/slice | solution.py:17
  106.0 2.1 %copy.13 = f32[32,10,10,1]{0,3,2,1:T(1,128)S(1)} copy(f32[32,10,10,1]{3,0,2,1:T(8,128)} %get-tuple-element.9) | data formatting | bytes 25600 | tf_op jit(solution)/shard_map/slice | solution.py:17
  109.4 2.1 %copy.15 = f32[32,10,10,1]{0,3,2,1:T(1,128)S(1)} copy(f32[32,10,10,1]{3,0,2,1:T(8,128)} %get-tuple-element.10) | data formatting | bytes 25600 | tf_op jit(solution)/shard_map/slice | solution.py:15
  111.5 4.6 %collective-permute-start.5 = (f32[32,10,10,1]{0,3,2,1:T(1,128)S(1)}, f32[32,10,10,1]{0,3,2,1:T(1,128)S(1)}, u32[]{:S(2)}, u32[]{:S(2)}) collective-permute-start(f32[32,10,10,1]{0,3,2,1:T(1,128)S(1)} %copy.15), channel_id=1, source_target_pairs={{0,1},{1,2},{2,3},{4,5},{5,6},{6,7},{8,9},{9,10},{10,11},{12,13},{... | collective-permute-start | bytes 38408 | tf_op jit(solution)/shard_map/ppermute | solution.py:14
  117.9 1.9 copy.16
  119.7 2.9 %fusion.17 = f32[32,8,8,128]{3,0,2,1:T(8,128)S(1)} fusion(f32[32,8,8,128]{3,0,2,1:T(8,128)S(1)} %get-tuple-element.26, f32[32,10,10,1]{3,0,2,1:T(8,128)} %copy.16, f32[32,10,1,128]{3,0,2,1:T(8,128)} %copy-done.5, f32[32,10,1,128]{3,0,2,1:T(8,128)} %copy-done.3, f32[32,1,8,128]{3,0,2,1:T(8,128)S(1)} %collective-permute-done, ...), kind=kLoop, calls=%fused_computation.58 | loop fusion | flops 6553600 | bytes 3793920 | tf_op jit(solution)/shard_map/div | solution.py:31
  122.7 3.7 %collective-permute-start.7 = (f32[32,1,8,128]{3,0,2,1:T(8,128)S(1)}, f32[32,1,8,128]{3,0,2,1:T(8,128)S(1)}, u32[]{:S(2)}, u32[]{:S(2)}) collective-permute-start(f32[32,1,8,128]{3,0,2,1:T(8,128)S(1)} %get-tuple-element.19), channel_id=1, source_target_pairs={{0,8},{8,16},{16,24},{1,9},{9,17},{17,25},{2,10},{10,18},{18,26},{... | collective-permute-start | bytes 393224 | tf_op jit(solution)/shard_map/ppermute | solution.py:14
  128.8 4.4 %collective-permute-done.6 = f32[32,1,8,128]{3,0,2,1:T(8,128)S(1)} collective-permute-done((f32[32,1,8,128]{3,0,2,1:T(8,128)S(1)}, f32[32,1,8,128]{3,0,2,1:T(8,128)S(1)}, u32[]{:S(2)}, u32[]{:S(2)}) %collective-permute-start.6) | collective-permute-done | bytes 131104 | tf_op jit(solution)/shard_map/ppermute | solution.py:17
  135.9 2.0 collective-permute-done.8
  138.7 2.3 %fusion.36 = (f32[32,10,10,1]{3,0,2,1:T(8,128)}, f32[32,10,10,1]{3,0,2,1:T(8,128)}) fusion(f32[32,10,10,128]{3,0,2,1:T(8,128)S(1)} %pad_maximum_fusion.1), kind=kLoop, calls=%fused_computation.110 | loop fusion | bytes 51200 | tf_op jit(solution)/shard_map/slice | solution.py:17
  140.9 2.1 %copy.17 = f32[32,10,10,1]{0,3,2,1:T(1,128)S(1)} copy(f32[32,10,10,1]{3,0,2,1:T(8,128)} %get-tuple-element.7) | data formatting | bytes 25600 | tf_op jit(solution)/shard_map/slice | solution.py:17
  144.3 2.1 %copy.19 = f32[32,10,10,1]{0,3,2,1:T(1,128)S(1)} copy(f32[32,10,10,1]{3,0,2,1:T(8,128)} %get-tuple-element.8) | data formatting | bytes 25600 | tf_op jit(solution)/shard_map/slice | solution.py:15
  146.4 4.8 %collective-permute-start.11 = (f32[32,10,10,1]{0,3,2,1:T(1,128)S(1)}, f32[32,10,10,1]{0,3,2,1:T(1,128)S(1)}, u32[]{:S(2)}, u32[]{:S(2)}) collective-permute-start(f32[32,10,10,1]{0,3,2,1:T(1,128)S(1)} %copy.19), channel_id=1, source_target_pairs={{0,1},{1,2},{2,3},{4,5},{5,6},{6,7},{8,9},{9,10},{10,11},{12,13},{... | collective-permute-start | bytes 38408 | tf_op jit(solution)/shard_map/ppermute | solution.py:14
  153.0 1.9 copy.20
  154.9 2.9 %fusion.10 = f32[32,8,8,128]{3,0,2,1:T(8,128)S(1)} fusion(f32[32,8,8,128]{3,0,2,1:T(8,128)S(1)} %get-tuple-element.26, f32[32,10,10,1]{3,0,2,1:T(8,128)} %copy.20, f32[32,10,1,128]{3,0,2,1:T(8,128)} %copy-done.6, f32[32,10,1,128]{3,0,2,1:T(8,128)} %copy-done.4, f32[32,1,8,128]{3,0,2,1:T(8,128)S(1)} %collective-permute-done.6, ...), kind=kLoop, calls=%fused_computation.33 | loop fusion | flops 6553600 | bytes 3793920 | tf_op jit(solution)/shard_map/div | solution.py:31
  157.8 2.8 %collective-permute-start.13 = (f32[32,1,8,128]{3,0,2,1:T(8,128)S(1)}, f32[32,1,8,128]{3,0,2,1:T(8,128)S(1)}, u32[]{:S(2)}, u32[]{:S(2)}) collective-permute-start(f32[32,1,8,128]{3,0,2,1:T(8,128)S(1)} %get-tuple-element.17), channel_id=1, source_target_pairs={{0,8},{8,16},{16,24},{1,9},{9,17},{17,25},{2,10},{10,18},{18,26},{... | collective-permute-start | bytes 393224 | tf_op jit(solution)/shard_map/ppermute | solution.py:14
  163.4 4.1 %collective-permute-done.12 = f32[32,1,8,128]{3,0,2,1:T(8,128)S(1)} collective-permute-done((f32[32,1,8,128]{3,0,2,1:T(8,128)S(1)}, f32[32,1,8,128]{3,0,2,1:T(8,128)S(1)}, u32[]{:S(2)}, u32[]{:S(2)}) %collective-permute-start.12) | collective-permute-done | bytes 131104 | tf_op jit(solution)/shard_map/ppermute | solution.py:17
  170.2 2.0 collective-permute-done.14
  172.8 2.2 %fusion.35 = (f32[32,10,10,1]{3,0,2,1:T(8,128)}, f32[32,10,10,1]{3,0,2,1:T(8,128)}) fusion(f32[32,10,10,128]{3,0,2,1:T(8,128)S(1)} %pad_maximum_fusion.2), kind=kLoop, calls=%fused_computation.109 | loop fusion | bytes 51200 | tf_op jit(solution)/shard_map/slice | solution.py:17
  175.1 2.1 %copy.21 = f32[32,10,10,1]{0,3,2,1:T(1,128)S(1)} copy(f32[32,10,10,1]{3,0,2,1:T(8,128)} %get-tuple-element.5) | data formatting | bytes 25600 | tf_op jit(solution)/shard_map/slice | solution.py:17
  178.6 2.7 %copy.23 = f32[32,10,10,1]{0,3,2,1:T(1,128)} copy(f32[32,10,10,1]{3,0,2,1:T(8,128)} %get-tuple-element.6) | data formatting | bytes 25600 | tf_op jit(solution)/shard_map/slice | solution.py:15
  181.3 5.5 %collective-permute-start.17 = (f32[32,10,10,1]{0,3,2,1:T(1,128)}, f32[32,10,10,1]{0,3,2,1:T(1,128)}, u32[]{:S(2)}, u32[]{:S(2)}) collective-permute-start(f32[32,10,10,1]{0,3,2,1:T(1,128)} %copy.23), channel_id=1, source_target_pairs={{0,1},{1,2},{2,3},{4,5},{5,6},{6,7},{8,9},{9,10},{10,11},{12,13},{... | collective-permute-start | bytes 38408 | tf_op jit(solution)/shard_map/ppermute | solution.py:14
  188.7 2.6 %copy.24 = f32[32,10,10,1]{3,0,2,1:T(8,128)} copy(f32[32,10,10,1]{0,3,2,1:T(1,128)} %collective-permute-done.17) | data formatting | bytes 25600 | tf_op jit(solution)/shard_map/ppermute | solution.py:14
  191.3 3.0 %fusion.3 = f32[32,8,8,128]{3,0,2,1:T(8,128)S(1)} fusion(f32[32,8,8,128]{3,0,2,1:T(8,128)S(1)} %get-tuple-element.26, f32[32,10,10,1]{3,0,2,1:T(8,128)} %copy.24, f32[32,10,1,128]{3,0,2,1:T(8,128)} %copy-done.8, f32[32,10,1,128]{3,0,2,1:T(8,128)} %copy-done.7, f32[32,1,8,128]{3,0,2,1:T(8,128)S(1)} %collective-permute-done.12, ...), kind=kLoop, calls=%fused_computation.8 | loop fusion | flops 6815744 | bytes 4842496 | tf_op jit(solution)/shard_map/add | solution.py:54
  (63 shorter events, 29.7 us)
Async XLA Ops:
  6.5 72.0 %all-gather.3.cloned.1.call-start = ((), (), s32[]{:S(2)}) async-start(), calls=%async_computation | async-start | bytes 4325376 | tf_op jit(solution)/shard_map/all_gather | solution.py:45
  8.4 5.7 %copy-start.10 = (f32[512]{0:T(512)S(1)}, f32[512]{0:T(512)}, u32[]{:S(2)}) copy-start(f32[512]{0:T(512)} %param.10) | copy-start | bytes 6148
  8.4 5.7 %copy-start.9 = (f32[8,8,128]{2,1,0:T(8,128)S(1)}, f32[8,8,128]{2,1,0:T(8,128)}, u32[]{:S(2)}) copy-start(f32[8,8,128]{2,1,0:T(8,128)} %param.11) | copy-start | bytes 98308
  78.6 2.6 %copy-start = (bf16[32,8,8,128]{3,2,1,0:T(8,128)(2,1)S(1)}, bf16[32,8,8,128]{3,2,1,0:T(8,128)(2,1)}, u32[]{:S(2)}) copy-start(bf16[32,8,8,128]{3,2,1,0:T(8,128)(2,1)} %param.7) | copy-start | bytes 1572868
  78.6 2.6 %copy-start.1 = (bf16[32,8,8,128]{3,2,1,0:T(8,128)(2,1)S(1)}, bf16[32,8,8,128]{3,2,1,0:T(8,128)(2,1)}, u32[]{:S(2)}) copy-start(bf16[32,8,8,128]{3,2,1,0:T(8,128)(2,1)} %param.6) | copy-start | bytes 1572868
  87.2 6.3 %collective-permute-start.1 = (f32[32,1,8,128]{3,0,2,1:T(8,128)S(1)}, f32[32,1,8,128]{3,0,2,1:T(8,128)S(1)}, u32[]{:S(2)}, u32[]{:S(2)}) collective-permute-start(f32[32,1,8,128]{3,0,2,1:T(8,128)S(1)} %get-tuple-element.21), channel_id=1, source_target_pairs={{0,8},{8,16},{16,24},{1,9},{9,17},{17,25},{2,10},{10,18},{18,26},{... | collective-permute-start | bytes 393224 | tf_op jit(solution)/shard_map/ppermute | solution.py:14
  90.4 8.1 %collective-permute-start = (f32[32,1,8,128]{3,0,2,1:T(8,128)S(1)}, f32[32,1,8,128]{3,0,2,1:T(8,128)S(1)}, u32[]{:S(2)}, u32[]{:S(2)}) collective-permute-start(f32[32,1,8,128]{3,0,2,1:T(8,128)S(1)} %get-tuple-element.22), channel_id=1, source_target_pairs={{8,0},{16,8},{24,16},{9,1},{17,9},{25,17},{10,2},{18,10},{26,18},{... | collective-permute-start | bytes 393224 | tf_op jit(solution)/shard_map/ppermute | solution.py:17
  98.5 2.6 %collective-permute-start.3 = (f32[32,10,1,128]{3,0,2,1:T(8,128)S(1)}, f32[32,10,1,128]{3,0,2,1:T(8,128)S(1)}, u32[]{:S(2)}, u32[]{:S(2)}) collective-permute-start(f32[32,10,1,128]{3,0,2,1:T(8,128)S(1)} %get-tuple-element.15), channel_id=1, source_target_pairs={{0,4},{1,5},{2,6},{3,7},{8,12},{9,13},{10,14},{11,15},{16,20},{17,... | collective-permute-start | bytes 491528 | tf_op jit(solution)/shard_map/ppermute | solution.py:14
  99.8 3.3 %collective-permute-start.2 = (f32[32,10,1,128]{3,0,2,1:T(8,128)S(1)}, f32[32,10,1,128]{3,0,2,1:T(8,128)S(1)}, u32[]{:S(2)}, u32[]{:S(2)}) collective-permute-start(f32[32,10,1,128]{3,0,2,1:T(8,128)S(1)} %get-tuple-element.16), channel_id=1, source_target_pairs={{4,0},{5,1},{6,2},{7,3},{12,8},{13,9},{14,10},{15,11},{20,16},{21,... | collective-permute-start | bytes 491528 | tf_op jit(solution)/shard_map/ppermute | solution.py:17
  101.1 2.2 %copy-start.3 = (f32[32,10,1,128]{3,0,2,1:T(8,128)}, f32[32,10,1,128]{3,0,2,1:T(8,128)S(1)}, u32[]{:S(2)}) copy-start(f32[32,10,1,128]{3,0,2,1:T(8,128)S(1)} %collective-permute-done.3) | copy-start | bytes 491524
  103.1 0.7 copy-start.5
  108.1 7.9 %collective-permute-start.4 = (f32[32,10,10,1]{0,3,2,1:T(1,128)S(1)}, f32[32,10,10,1]{0,3,2,1:T(1,128)S(1)}, u32[]{:S(2)}, u32[]{:S(2)}) collective-permute-start(f32[32,10,10,1]{0,3,2,1:T(1,128)S(1)} %copy.13), channel_id=1, source_target_pairs={{1,0},{2,1},{3,2},{5,4},{6,5},{7,6},{9,8},{10,9},{11,10},{13,12},{... | collective-permute-start | bytes 38408 | tf_op jit(solution)/shard_map/ppermute | solution.py:17
  111.5 6.4 %collective-permute-start.5 = (f32[32,10,10,1]{0,3,2,1:T(1,128)S(1)}, f32[32,10,10,1]{0,3,2,1:T(1,128)S(1)}, u32[]{:S(2)}, u32[]{:S(2)}) collective-permute-start(f32[32,10,10,1]{0,3,2,1:T(1,128)S(1)} %copy.15), channel_id=1, source_target_pairs={{0,1},{1,2},{2,3},{4,5},{5,6},{6,7},{8,9},{9,10},{10,11},{12,13},{... | collective-permute-start | bytes 38408 | tf_op jit(solution)/shard_map/ppermute | solution.py:14
  122.7 6.2 %collective-permute-start.7 = (f32[32,1,8,128]{3,0,2,1:T(8,128)S(1)}, f32[32,1,8,128]{3,0,2,1:T(8,128)S(1)}, u32[]{:S(2)}, u32[]{:S(2)}) collective-permute-start(f32[32,1,8,128]{3,0,2,1:T(8,128)S(1)} %get-tuple-element.19), channel_id=1, source_target_pairs={{0,8},{8,16},{16,24},{1,9},{9,17},{17,25},{2,10},{10,18},{18,26},{... | collective-permute-start | bytes 393224 | tf_op jit(solution)/shard_map/ppermute | solution.py:14
  126.3 6.9 %collective-permute-start.6 = (f32[32,1,8,128]{3,0,2,1:T(8,128)S(1)}, f32[32,1,8,128]{3,0,2,1:T(8,128)S(1)}, u32[]{:S(2)}, u32[]{:S(2)}) collective-permute-start(f32[32,1,8,128]{3,0,2,1:T(8,128)S(1)} %get-tuple-element.20), channel_id=1, source_target_pairs={{8,0},{16,8},{24,16},{9,1},{17,9},{25,17},{10,2},{18,10},{26,18},{... | collective-permute-start | bytes 393224 | tf_op jit(solution)/shard_map/ppermute | solution.py:17
  133.2 2.6 %collective-permute-start.9 = (f32[32,10,1,128]{3,0,2,1:T(8,128)S(1)}, f32[32,10,1,128]{3,0,2,1:T(8,128)S(1)}, u32[]{:S(2)}, u32[]{:S(2)}) collective-permute-start(f32[32,10,1,128]{3,0,2,1:T(8,128)S(1)} %get-tuple-element.13), channel_id=1, source_target_pairs={{0,4},{1,5},{2,6},{3,7},{8,12},{9,13},{10,14},{11,15},{16,20},{17,... | collective-permute-start | bytes 491528 | tf_op jit(solution)/shard_map/ppermute | solution.py:14
  134.5 3.3 %collective-permute-start.8 = (f32[32,10,1,128]{3,0,2,1:T(8,128)S(1)}, f32[32,10,1,128]{3,0,2,1:T(8,128)S(1)}, u32[]{:S(2)}, u32[]{:S(2)}) collective-permute-start(f32[32,10,1,128]{3,0,2,1:T(8,128)S(1)} %get-tuple-element.14), channel_id=1, source_target_pairs={{4,0},{5,1},{6,2},{7,3},{12,8},{13,9},{14,10},{15,11},{20,16},{21,... | collective-permute-start | bytes 491528 | tf_op jit(solution)/shard_map/ppermute | solution.py:17
  135.8 2.0 copy-start.4
  137.8 0.7 copy-start.6
  143.0 8.2 %collective-permute-start.10 = (f32[32,10,10,1]{0,3,2,1:T(1,128)S(1)}, f32[32,10,10,1]{0,3,2,1:T(1,128)S(1)}, u32[]{:S(2)}, u32[]{:S(2)}) collective-permute-start(f32[32,10,10,1]{0,3,2,1:T(1,128)S(1)} %copy.17), channel_id=1, source_target_pairs={{1,0},{2,1},{3,2},{5,4},{6,5},{7,6},{9,8},{10,9},{11,10},{13,12},{... | collective-permute-start | bytes 38408 | tf_op jit(solution)/shard_map/ppermute | solution.py:17
  146.4 6.6 %collective-permute-start.11 = (f32[32,10,10,1]{0,3,2,1:T(1,128)S(1)}, f32[32,10,10,1]{0,3,2,1:T(1,128)S(1)}, u32[]{:S(2)}, u32[]{:S(2)}) collective-permute-start(f32[32,10,10,1]{0,3,2,1:T(1,128)S(1)} %copy.19), channel_id=1, source_target_pairs={{0,1},{1,2},{2,3},{4,5},{5,6},{6,7},{8,9},{9,10},{10,11},{12,13},{... | collective-permute-start | bytes 38408 | tf_op jit(solution)/shard_map/ppermute | solution.py:14
  157.8 5.6 %collective-permute-start.13 = (f32[32,1,8,128]{3,0,2,1:T(8,128)S(1)}, f32[32,1,8,128]{3,0,2,1:T(8,128)S(1)}, u32[]{:S(2)}, u32[]{:S(2)}) collective-permute-start(f32[32,1,8,128]{3,0,2,1:T(8,128)S(1)} %get-tuple-element.17), channel_id=1, source_target_pairs={{0,8},{8,16},{16,24},{1,9},{9,17},{17,25},{2,10},{10,18},{18,26},{... | collective-permute-start | bytes 393224 | tf_op jit(solution)/shard_map/ppermute | solution.py:14
  160.6 6.9 %collective-permute-start.12 = (f32[32,1,8,128]{3,0,2,1:T(8,128)S(1)}, f32[32,1,8,128]{3,0,2,1:T(8,128)S(1)}, u32[]{:S(2)}, u32[]{:S(2)}) collective-permute-start(f32[32,1,8,128]{3,0,2,1:T(8,128)S(1)} %get-tuple-element.18), channel_id=1, source_target_pairs={{8,0},{16,8},{24,16},{9,1},{17,9},{25,17},{10,2},{18,10},{26,18},{... | collective-permute-start | bytes 393224 | tf_op jit(solution)/shard_map/ppermute | solution.py:17
  167.5 2.6 %collective-permute-start.15 = (f32[32,10,1,128]{3,0,2,1:T(8,128)S(1)}, f32[32,10,1,128]{3,0,2,1:T(8,128)S(1)}, u32[]{:S(2)}, u32[]{:S(2)}) collective-permute-start(f32[32,10,1,128]{3,0,2,1:T(8,128)S(1)} %get-tuple-element.11), channel_id=1, source_target_pairs={{0,4},{1,5},{2,6},{3,7},{8,12},{9,13},{10,14},{11,15},{16,20},{17,... | collective-permute-start | bytes 491528 | tf_op jit(solution)/shard_map/ppermute | solution.py:14
  168.9 3.3 %collective-permute-start.14 = (f32[32,10,1,128]{3,0,2,1:T(8,128)S(1)}, f32[32,10,1,128]{3,0,2,1:T(8,128)S(1)}, u32[]{:S(2)}, u32[]{:S(2)}) collective-permute-start(f32[32,10,1,128]{3,0,2,1:T(8,128)S(1)} %get-tuple-element.12), channel_id=1, source_target_pairs={{4,0},{5,1},{6,2},{7,3},{12,8},{13,9},{14,10},{15,11},{20,16},{21,... | collective-permute-start | bytes 491528 | tf_op jit(solution)/shard_map/ppermute | solution.py:17
  170.2 2.2 %copy-start.7 = (f32[32,10,1,128]{3,0,2,1:T(8,128)}, f32[32,10,1,128]{3,0,2,1:T(8,128)S(1)}, u32[]{:S(2)}) copy-start(f32[32,10,1,128]{3,0,2,1:T(8,128)S(1)} %collective-permute-done.15) | copy-start | bytes 491524
  172.1 0.7 copy-start.8
  177.1 9.7 %collective-permute-start.16 = (f32[32,10,10,1]{0,3,2,1:T(1,128)S(1)}, f32[32,10,10,1]{0,3,2,1:T(1,128)S(1)}, u32[]{:S(2)}, u32[]{:S(2)}) collective-permute-start(f32[32,10,10,1]{0,3,2,1:T(1,128)S(1)} %copy.21), channel_id=1, source_target_pairs={{1,0},{2,1},{3,2},{5,4},{6,5},{7,6},{9,8},{10,9},{11,10},{13,12},{... | collective-permute-start | bytes 38408 | tf_op jit(solution)/shard_map/ppermute | solution.py:17
  181.3 10.0 %copy-start.2 = (f32[32,8,8,128]{3,2,1,0:T(8,128)S(1)}, f32[32,8,8,128]{3,2,1,0:T(8,128)}, u32[]{:S(2)}) copy-start(f32[32,8,8,128]{3,2,1,0:T(8,128)} %param.8) | copy-start | bytes 3145732
  181.3 7.4 %collective-permute-start.17 = (f32[32,10,10,1]{0,3,2,1:T(1,128)}, f32[32,10,10,1]{0,3,2,1:T(1,128)}, u32[]{:S(2)}, u32[]{:S(2)}) collective-permute-start(f32[32,10,10,1]{0,3,2,1:T(1,128)} %copy.23), channel_id=1, source_target_pairs={{0,1},{1,2},{2,3},{4,5},{5,6},{6,7},{8,9},{9,10},{10,11},{12,13},{... | collective-permute-start | bytes 38408 | tf_op jit(solution)/shard_map/ppermute | solution.py:14
Sparse Core Ops, SparseCore 0:
  14.2 64.3 all-gather.2
